TPU v7x, 32 devices: a whole 2x2x4 slice. The times are simulated.
32 devices in a mesh: node: 4 (over y, x), space: 8 (over z, core).
Axes of the slice: x: 2, y: 2, z: 4, core: 2. Of those that a mesh axis runs over, the one named last changes fastest.
Arguments:
- initial: float32 [2, 512, 4096], P(None, 'space'), may hold values from 0 to 1
- sections: float32 [4, 2, 512, 4096], P('node', None, 'space'), may hold values from 0 to 1
- feed_rate: float32 [512, 4096], P('space'), may hold values from 0.02 to 0.12
- kill_rate: float32 [512, 4096], P('space'), may hold values from 0.04 to 0.12
Outputs:
- new_sections: float32 [4, 2, 512, 4096], P('node', None, 'space')
- residual_max: float32 [], replicated
All inputs are finite; a program needn't handle non-finite values.
Results may differ from a plain program's by a relative error of at most 0.000094.
Values sent between devices are 32-bit elements; how exact they have to be, the bound alone decides.
A program may use at most 64 MiB of HBM per device.

v0:
```python
import functools

import jax
import jax.numpy as jnp
import numpy as np
from jax import lax
from jax.experimental import pallas as pl
from jax.experimental.pallas import tpu as pltpu
from jax.sharding import PartitionSpec as P

SWEEPS = 6


step_size = 4.0
diff_u = 1.0
diff_v = 0.5


def radau_target(order, value):
    before = 1.0
    current = value
    previous = 1.0
    for degree in range(1, order):
        following = ((2 * degree + 1) * value * current - degree * before) / (degree + 1)
        before = current
        current = following
    previous = before
    return current - previous


def radau_table(total):
    grid_count = 20000
    roots_found = []
    left_value = -1.0
    left_target = radau_target(total, left_value)
    for step_index in range(1, grid_count):
        right_value = -1.0 + 2.0 * step_index / grid_count
        right_target = radau_target(total, right_value)
        if left_target * right_target < 0.0:
            lower = left_value
            upper = right_value
            lower_target = left_target
            for bisect_index in range(80):
                halfway = 0.5 * (lower + upper)
                halfway_target = radau_target(total, halfway)
                if lower_target * halfway_target <= 0.0:
                    upper = halfway
                else:
                    lower = halfway
                    lower_target = halfway_target
            roots_found.append(0.5 * (lower + upper))
        left_value = right_value
        left_target = right_target
    roots_found.append(1.0)
    points = [(value + 1.0) / 2.0 for value in roots_found]
    quad_rows = []
    for node_index in range(total):
        row_values = []
        for basis_index in range(total):
            coefs = [1.0]
            for other_index in range(total):
                if other_index != basis_index:
                    scale = 1.0 / (points[basis_index] - points[other_index])
                    shifted = [0.0] + coefs
                    widened = coefs + [0.0]
                    coefs = [
                        (shifted[k] - points[other_index] * widened[k]) * scale
                        for k in range(len(shifted))
                    ]
            integral = 0.0
            for power_index in range(len(coefs)):
                integral += (
                    coefs[power_index] * points[node_index] ** (power_index + 1) / (power_index + 1)
                )
            row_values.append(integral)
        quad_rows.append(row_values)
    return (np.array(points), np.array(quad_rows))


MESH = pl.DeviceIdType.MESH
LANES = 128
EDGE = 8
TOP = 2 * EDGE
SLOPE_TILES = 2
MIX_TILES = 2
GATHER_TILES = 4
LATE = 16


def grouped(total, most):
    return max(k for k in range(1, most + 1) if total % k == 0)


def kernel(
    nodes,
    spaces,
    table,
    sections,
    feed_rate,
    kill_rate,
    initial,
    out,
    residual,
    sec,
    feed,
    kill,
    init,
    side,
    slope,
    arrived,
    mixed,
    quad,
    works_a,
    works_b,
    works_c,
    works_d,
    works_e,
    peak,
    peaks_node,
    peaks_space,
    local_sem,
    halo_sem,
    first_sem,
    second_sem,
    side_sem,
    peak_node_sem,
    peak_space_sem,
):
    works = (works_a, works_b, works_c, works_d, works_e)
    cols = sec.shape[1]
    rows = slope.shape[2]
    block = cols // nodes
    me = lax.axis_index("node")
    here = lax.axis_index("space")
    tall = 2 if nodes % 2 == 0 else 1
    wide = nodes // tall
    early = rows - 2 * EDGE - LATE
    pieces = (
        (EDGE, early),
        (EDGE + early, LATE),
        (0, EDGE),
        (rows - EDGE, EDGE),
    )
    mids, edges = (0, 1), (2, 3)

    def ahead(o):
        return ((me // wide + o // wide) % tall) * wide + (me % wide + o % wide) % wide

    def behind(o):
        return ((me // wide + tall - o // wide) % tall) * wide + (
            me % wide + wide - o % wide
        ) % wide

    def fetch(source, target, offset, sem):
        for k in range(rows // EDGE):
            pltpu.make_async_copy(
                source.at[k], target.at[:, pl.ds(offset + k * EDGE, EDGE)], sem
            ).start()

    own_rows = pl.ds(TOP, rows)
    for s in range(2):
        fetch(sections.at[s], sec.at[s], TOP, local_sem.at[s])
    fetch(feed_rate, feed, 0, local_sem.at[2])
    fetch(kill_rate, kill, 0, local_sem.at[3])

    barrier = pltpu.get_barrier_semaphore()
    for o in range(1, nodes):
        pl.semaphore_signal(barrier, inc=1, device_id={"node": ahead(o)}, device_id_type=MESH)
    for o in range(1, spaces):
        pl.semaphore_signal(
            barrier, inc=1, device_id={"space": (here + o) % spaces}, device_id_type=MESH
        )

    def arrived_in(ref, sem):
        pltpu.make_async_copy(ref, ref, sem).wait()

    def halo(ref, sem, s, way):
        start = TOP + rows - EDGE if way == 0 else TOP
        land = TOP - EDGE if way == 0 else TOP + rows
        other = (here + 1) % spaces if way == 0 else (here + spaces - 1) % spaces
        return pltpu.make_async_remote_copy(
            src_ref=ref.at[s, :, pl.ds(start, EDGE)],
            dst_ref=ref.at[s, :, pl.ds(land, EDGE)],
            send_sem=sem.at[0, s, way],
            recv_sem=sem.at[1, s, way],
            device_id={"space": other},
            device_id_type=MESH,
        )

    def first(s, p, o):
        start, size = pieces[p]
        return pltpu.make_async_remote_copy(
            src_ref=slope.at[s, pl.ds(ahead(o) * block, block), pl.ds(start, size)],
            dst_ref=arrived.at[o - 1, s, :, pl.ds(start, size)],
            send_sem=first_sem.at[0, s, p, o - 1],
            recv_sem=first_sem.at[1, s, p, o - 1],
            device_id={"node": ahead(o)},
            device_id_type=MESH,
        )

    def second(s, p, o):
        start, size = pieces[p]
        return pltpu.make_async_remote_copy(
            src_ref=mixed.at[o - 1, s, :, pl.ds(start, size)],
            dst_ref=quad.at[s, pl.ds(me * block, block), pl.ds(start, size)],
            send_sem=second_sem.at[0, s, p, o - 1],
            recv_sem=second_sem.at[1, s, p, o - 1],
            device_id={"node": ahead(o)},
            device_id_type=MESH,
        )

    arrived_in(sec.at[0, :, own_rows], local_sem.at[0])
    arrived_in(sec.at[1, :, own_rows], local_sem.at[1])
    pl.semaphore_wait(barrier, nodes - 1 + spaces - 1)
    for s in range(2):
        for way in range(2):
            halo(sec, halo_sem, s, way).start()
    arrived_in(feed, local_sem.at[2])
    arrived_in(kill, local_sem.at[3])
    for s in range(2):
        fetch(initial.at[s], init.at[s], 0, local_sem.at[4 + s])

    own_step = table[nodes * nodes + me]
    coupling = (own_step * diff_u, own_step * diff_v)

    def around(ref, s, c, count, start, size):
        lane = lax.broadcasted_iota(jnp.int32, (size, LANES), 1)
        at = pl.ds(start, size)
        where = [(c + cols - 1) % cols] + [c + k for k in range(count)] + [(c + count) % cols]
        tiles = [ref[s, k, at, :] for k in where]
        sums = []
        for k in range(1, count + 1):
            left = pltpu.roll(jnp.where(lane == LANES - 1, tiles[k - 1], tiles[k]), 1, 1)
            right = pltpu.roll(jnp.where(lane == 0, tiles[k + 1], tiles[k]), LANES - 1, 1)
            below = ref[s, where[k], pl.ds(start + 1, size), :]
            above = ref[s, where[k], pl.ds(start - 1, size), :]
            sums.append((below + above) + (right + left))
        return tiles[1:-1], sums

    def slopes(owner, p):
        start, size = pieces[p]
        at = pl.ds(start, size)
        group = grouped(block, SLOPE_TILES if size > EDGE else 8)

        def one(g, carry):
            c = owner * block + g * group
            us, u_rings = around(sec, 0, c, group, TOP + start, size)
            vs, v_rings = around(sec, 1, c, group, TOP + start, size)
            for k in range(group):
                u, v = us[k], vs[k]
                f = feed[c + k, at, :]
                u_lap = diff_u * (u_rings[k] - 4.0 * u)
                v_lap = diff_v * (v_rings[k] - 4.0 * v)
                product = u * v * v
                slope[0, c + k, at, :] = u_lap + (f * (1.0 - u) - product)
                slope[1, c + k, at, :] = v_lap + (product - (f + kill[c + k, at, :]) * v)
                side[0, c + k, pl.ds(TOP + start, size), :] = own_step * u_lap
                side[1, c + k, pl.ds(TOP + start, size), :] = own_step * v_lap
            return carry

        lax.fori_loop(0, block // group, one, 0)

    order = tuple(range(nodes - 1, 0, -1))
    for o in order:
        for p in mids:
            slopes(ahead(o), p)
            first(0, p, o).start()
    for s in range(2):
        for way in range(2):
            halo(sec, halo_sem, s, way).wait_recv()
    for o in order:
        for p in edges:
            slopes(ahead(o), p)
            first(0, p, o).start()
    for o in order:
        for p in mids:
            first(1, p, o).start()
    for o in order:
        for p in edges:
            first(1, p, o).start()
    for p in mids + edges:
        slopes(me, p)

    sources = [me] + [behind(o) for o in range(1, nodes)]
    targets = [me] + [ahead(o) for o in range(1, nodes)]
    weights = [[table[m * nodes + j] for j in sources] for m in targets]

    def mix(s, p):
        start, size = pieces[p]
        at = pl.ds(start, size)
        group = grouped(block, MIX_TILES if size > EDGE else 8)

        def one(g, carry):
            for i in range(group):
                k = g * group + i
                values = [slope[s, me * block + k, at, :]] + [
                    arrived[o - 1, s, k, at, :] for o in range(1, nodes)
                ]
                for t, weight in enumerate(weights):
                    total = weight[0] * values[0]
                    for j in range(1, nodes):
                        total = total + weight[j] * values[j]
                    if t == 0:
                        quad[s, me * block + k, at, :] = total
                    else:
                        mixed[t - 1, s, k, at, :] = total
            return carry

        lax.fori_loop(0, block // group, one, 0)

    for s in range(2):
        for o in order:
            for p in edges + mids:
                first(s, p, o).wait_recv()
        for p in edges + mids:
            mix(s, p)
            for o in order:
                second(s, p, o).start()

    inverse = [1.0 / (4.0 * c + 1.0) for c in coupling]

    def gather(s, p, worst):
        start, size = pieces[p]
        at = pl.ds(start, size)
        for o in order:
            second(s, p, o).wait_recv()

        group = grouped(cols, GATHER_TILES if size > EDGE else 8)
        where = pl.ds(TOP + start, size)

        def one(g, worst):
            for k in range(group):
                c = g * group + k
                whole = init[s, c, at, :] + quad[s, c, at, :]
                gap = jnp.abs(whole - sec[s, c, where, :])
                side[s, c, where, :] = (whole - side[s, c, where, :]) * inverse[s]
                worst = jnp.maximum(worst, jnp.max(gap.reshape(size // EDGE, EDGE, LANES), axis=0))
            return worst

        return lax.fori_loop(0, cols // group, one, worst)

    bottom = TOP + rows + SWEEPS - 1
    split = bottom - 2 * LATE

    def band(s, i):
        factor = coupling[s] * inverse[s]
        for k in range(SWEEPS):
            start = TOP - SWEEPS + 1 + k if i == 0 else split - k
            stop = split - k if i == 0 else bottom - k
            source, plane = (sec, s) if k == 0 else (works[k - 1], 0)
            for low in range(start, stop, EDGE):
                size = min(EDGE, stop - low)
                _, sums = around(source, plane, 0, cols, low, size)
                for c in range(cols):
                    value = side[s, c, pl.ds(low, size), :] + factor * sums[c]
                    if k == SWEEPS - 1:
                        out[s, (low - TOP) // EDGE, c] = value
                    else:
                        works[k][0, c, pl.ds(low, size), :] = value

    def peak_node(o):
        return pltpu.make_async_remote_copy(
            src_ref=peak.at[0],
            dst_ref=peaks_node.at[o - 1],
            send_sem=peak_node_sem.at[0, o - 1],
            recv_sem=peak_node_sem.at[1, o - 1],
            device_id={"node": ahead(o)},
            device_id_type=MESH,
        )

    def peak_space(o):
        return pltpu.make_async_remote_copy(
            src_ref=peak.at[1],
            dst_ref=peaks_space.at[o - 1],
            send_sem=peak_space_sem.at[0, o - 1],
            recv_sem=peak_space_sem.at[1, o - 1],
            device_id={"space": (here + o) % spaces},
            device_id_type=MESH,
        )

    def fold_node():
        for o in range(1, nodes):
            peak_node(o).wait_recv()
        peak[1] = jnp.maximum(peak[0], jnp.max(peaks_node[...], axis=0))
        for o in range(1, spaces):
            peak_space(o).start()

    worst = jnp.zeros((EDGE, LANES), jnp.float32)
    for s in range(2):
        arrived_in(init.at[s], local_sem.at[4 + s])
        for p in edges:
            worst = gather(s, p, worst)
        for way in range(2):
            halo(side, side_sem, s, way).start()
        worst = gather(s, mids[0], worst)
        for way in range(2):
            halo(side, side_sem, s, way).wait_recv()
        band(s, 0)
        worst = gather(s, mids[1], worst)
        if s == 1:
            peak[0] = worst
            for o in range(1, nodes):
                peak_node(o).start()
        band(s, 1)
        if s == 1:
            fold_node()

    for o in range(1, spaces):
        peak_space(o).wait_recv()
    residual[0, 0] = jnp.max(jnp.maximum(peak[1], jnp.max(peaks_space[...], axis=0)))
    for s in range(2):
        for way in range(2):
            halo(sec, halo_sem, s, way).wait_send()
            halo(side, side_sem, s, way).wait_send()
        for p in mids + edges:
            for o in order:
                first(s, p, o).wait_send()
                second(s, p, o).wait_send()
    for o in range(1, nodes):
        peak_node(o).wait_send()
    for o in range(1, spaces):
        peak_space(o).wait_send()


def shards(initial, sections, feed_rate, kill_rate):
    nodes = lax.axis_size("node")
    spaces = lax.axis_size("space")
    rows, columns = feed_rate.shape
    cols = columns // LANES
    block = cols // nodes
    points, quad_matrix = radau_table(nodes)
    table = np.concatenate(
        [
            step_size * np.float32(quad_matrix).reshape(-1),
            step_size * np.float32(points),
        ]
    ).astype(np.float32)
    high = TOP + rows + TOP
    f32 = jnp.float32

    def tiled(array):
        split = array.reshape(*array.shape[:-2], rows // EDGE, EDGE, cols, LANES)
        return jnp.swapaxes(split, -3, -2)

    any_spec = pl.BlockSpec(memory_space=pl.ANY)
    result, residual = pl.pallas_call(
        functools.partial(kernel, nodes, spaces),
        out_shape=(
            pltpu.VMEM((2, rows // EDGE, cols, EDGE, LANES), f32),
            jax.ShapeDtypeStruct((1, 1), f32),
        ),
        in_specs=[pl.BlockSpec(memory_space=pltpu.SMEM)] + [any_spec] * 4,
        out_specs=(pl.BlockSpec(memory_space=pltpu.VMEM), pl.BlockSpec(memory_space=pltpu.SMEM)),
        scratch_shapes=[
            pltpu.VMEM((2, cols, high, LANES), f32),
            pltpu.VMEM((cols, rows, LANES), f32),
            pltpu.VMEM((cols, rows, LANES), f32),
            pltpu.VMEM((2, cols, rows, LANES), f32),
            pltpu.VMEM((2, cols, high, LANES), f32),
            pltpu.VMEM((2, cols, rows, LANES), f32),
            pltpu.VMEM((nodes - 1, 2, block, rows, LANES), f32),
            pltpu.VMEM((nodes - 1, 2, block, rows, LANES), f32),
            pltpu.VMEM((2, cols, rows, LANES), f32),
            *[pltpu.VMEM((1, cols, high, LANES), f32)] * (SWEEPS - 1),
            pltpu.VMEM((2, EDGE, LANES), f32),
            pltpu.VMEM((nodes - 1, EDGE, LANES), f32),
            pltpu.VMEM((spaces - 1, EDGE, LANES), f32),
            pltpu.SemaphoreType.DMA((6,)),
            pltpu.SemaphoreType.DMA((2, 2, 2)),
            pltpu.SemaphoreType.DMA((2, 2, 4, nodes - 1)),
            pltpu.SemaphoreType.DMA((2, 2, 4, nodes - 1)),
            pltpu.SemaphoreType.DMA((2, 2, 2)),
            pltpu.SemaphoreType.DMA((2, nodes - 1)),
            pltpu.SemaphoreType.DMA((2, spaces - 1)),
        ],
        compiler_params=pltpu.CompilerParams(
            collective_id=0, has_side_effects=True, vmem_limit_bytes=61 * 1024 * 1024
        ),
    )(jnp.asarray(table), *[tiled(a) for a in (sections[0], feed_rate, kill_rate, initial)])
    result = jnp.swapaxes(result, -3, -2).reshape(sections.shape)
    return (result, residual.reshape(()))


def solution(mesh):
    placed = (
        P(None, "space", None),
        P("node", None, "space", None),
        P("space", None),
        P("space", None),
    )
    return jax.shard_map(
        shards,
        mesh=mesh,
        in_specs=placed,
        out_specs=(P("node", None, "space", None), P()),
        check_vma=False,
    )
```

profile of v0, /device:TPU:0, one launch (start us, length us, event | category | flops | bytes accessed | tf_op | source)
XLA Modules:
  0.0 66.1 jit_solution(12029622887449511898)
XLA Ops:
  0.6 62.5 %shard_map.68 = (f32[2,8,32,8,128]{4,3,2,1,0:T(8,128)S(1)}, f32[1,1]{1,0:T(1,128)}) custom-call(f32[20]{0:T(128)} %constant.2.clone.table, f32[2,8,32,8,128]{4,3,2,1,0:T(8,128)} %bitcast.17, f32[8,32,8,128]{3,2,1,0:T(8,128)} %bitcast.19, f32[8,32,8,128]{3,2,1,0:T(8,128)} %bitcast.20, f32[2,8,32,8,128]{4,3,2,1,0:T(8,128)} %bitcast.18), custom_call_target="tpu_custom_call" | custom-call | tf_op jit(solution)/shard_map/pallas_call | solution.py:446
  63.1 1.3 %copy.9 = f32[1,2,64,4096]{3,2,1,0:T(8,128)} copy(f32[1,2,64,4096]{3,2,1,0:T(8,128)S(1)} %bitcast.16) | data formatting | bytes 4194304
where the time goes:
time: 66.3 us; the launch traced here: 66.1 us
  Pallas kernels  62.5 us (94%)
  between operations  2.33 us (4%)
  local copies, waits for them, and re-layouts  1.32 us (2%)
    pallas_call x1, Pallas kernels, shards(): pl.pallas_call(functools.partial(kernel, nodes, spaces), out_shape=(pltpu...  62.5 us

commit v1 on v0

v1 whole, which is shorter than its diff:
```python
import functools

import jax
import jax.numpy as jnp
import numpy as np
from jax import lax
from jax.experimental import pallas as pl
from jax.experimental.pallas import tpu as pltpu
from jax.sharding import PartitionSpec as P

SWEEPS = 6


step_size = 4.0
diff_u = 1.0
diff_v = 0.5


def radau_target(order, value):
    before = 1.0
    current = value
    previous = 1.0
    for degree in range(1, order):
        following = ((2 * degree + 1) * value * current - degree * before) / (degree + 1)
        before = current
        current = following
    previous = before
    return current - previous


def radau_table(total):
    grid_count = 20000
    roots_found = []
    left_value = -1.0
    left_target = radau_target(total, left_value)
    for step_index in range(1, grid_count):
        right_value = -1.0 + 2.0 * step_index / grid_count
        right_target = radau_target(total, right_value)
        if left_target * right_target < 0.0:
            lower = left_value
            upper = right_value
            lower_target = left_target
            for bisect_index in range(80):
                halfway = 0.5 * (lower + upper)
                halfway_target = radau_target(total, halfway)
                if lower_target * halfway_target <= 0.0:
                    upper = halfway
                else:
                    lower = halfway
                    lower_target = halfway_target
            roots_found.append(0.5 * (lower + upper))
        left_value = right_value
        left_target = right_target
    roots_found.append(1.0)
    points = [(value + 1.0) / 2.0 for value in roots_found]
    quad_rows = []
    for node_index in range(total):
        row_values = []
        for basis_index in range(total):
            coefs = [1.0]
            for other_index in range(total):
                if other_index != basis_index:
                    scale = 1.0 / (points[basis_index] - points[other_index])
                    shifted = [0.0] + coefs
                    widened = coefs + [0.0]
                    coefs = [
                        (shifted[k] - points[other_index] * widened[k]) * scale
                        for k in range(len(shifted))
                    ]
            integral = 0.0
            for power_index in range(len(coefs)):
                integral += (
                    coefs[power_index] * points[node_index] ** (power_index + 1) / (power_index + 1)
                )
            row_values.append(integral)
        quad_rows.append(row_values)
    return (np.array(points), np.array(quad_rows))


MESH = pl.DeviceIdType.MESH
LANES = 128
EDGE = 8
TOP = 2 * EDGE


def kernel(
    nodes,
    spaces,
    table,
    sections,
    feed_rate,
    kill_rate,
    initial,
    out,
    residual,
    sec,
    feed,
    kill,
    init,
    other,
    pack_out,
    pack_in,
    mixed,
    side,
    works_a,
    works_b,
    works_c,
    works_d,
    works_e,
    peak,
    peaks_node,
    peaks_space,
    local_sem,
    halo_sem,
    other_sem,
    pack_sem,
    first_sem,
    second_sem,
    side_sem,
    peak_node_sem,
    peak_space_sem,
):
    works = (works_a, works_b, works_c, works_d, works_e)
    cols = sec.shape[1]
    rows = feed.shape[1]
    block = cols // nodes
    me = lax.axis_index("node")
    here = lax.axis_index("space")
    tall = 2 if nodes % 2 == 0 else 1
    wide = nodes // tall
    chunks = (
        (0, TOP),
        (rows - TOP, TOP),
        (TOP, rows - 5 * EDGE),
        (rows - 3 * EDGE, EDGE),
    )
    pieces = (
        (0, EDGE),
        (rows - EDGE, EDGE),
        (EDGE, rows - 5 * EDGE),
        (rows - 4 * EDGE, 2 * EDGE),
        (rows - 2 * EDGE, EDGE),
    )
    own = me * block

    def ahead(o):
        return ((me // wide + o // wide) % tall) * wide + (me % wide + o % wide) % wide

    def negated(o):
        return ((tall - o // wide) % tall) * wide + (wide - o % wide) % wide

    def fetch(source, target, start, size, offset, sem):
        for k in range(start // EDGE, (start + size) // EDGE):
            pltpu.make_async_copy(
                source.at[k], target.at[:, pl.ds(offset + k * EDGE, EDGE)], sem
            ).start()

    def arrived_in(ref, sem):
        pltpu.make_async_copy(ref, ref, sem).wait()

    for i, (start, size) in enumerate(chunks):
        for s in range(2):
            fetch(sections.at[s], sec.at[s], start, size, TOP, local_sem.at[i])

    barrier = pltpu.get_barrier_semaphore()
    for o in range(1, nodes):
        pl.semaphore_signal(barrier, inc=1, device_id={"node": ahead(o)}, device_id_type=MESH)
    for o in range(1, spaces):
        pl.semaphore_signal(
            barrier, inc=1, device_id={"space": (here + o) % spaces}, device_id_type=MESH
        )

    mine = pl.ds(own, block)
    fetch(feed_rate.at[:, mine], feed, 0, rows, 0, local_sem.at[4])
    fetch(kill_rate.at[:, mine], kill, 0, rows, 0, local_sem.at[5])
    for s in range(2):
        fetch(initial.at[s, :, mine], init.at[s], 0, rows, 0, local_sem.at[6])

    def along(ref, sem, way):
        start = TOP + rows - EDGE if way == 0 else TOP
        land = TOP - EDGE if way == 0 else TOP + rows
        target = (here + 1) % spaces if way == 0 else (here + spaces - 1) % spaces
        return pltpu.make_async_remote_copy(
            src_ref=ref.at[:, pl.ds(start, EDGE)],
            dst_ref=ref.at[:, pl.ds(land, EDGE)],
            send_sem=sem.at[0, way],
            recv_sem=sem.at[1, way],
            device_id={"space": target},
            device_id_type=MESH,
        )

    def halo(ref, sem, s, way):
        return along(ref.at[s], sem.at[s], way)

    def forward(o, s, way):
        return along(other.at[o - 1, s, pl.ds(1, block)], other_sem.at[o - 1, s], way)

    def first(p, o):
        start, size = chunks[p]
        where = pl.ds(TOP + start, size)
        return pltpu.make_async_remote_copy(
            src_ref=sec.at[:, pl.ds(ahead(o) * block, block), where],
            dst_ref=other.at[o - 1, :, pl.ds(1, block), where],
            send_sem=first_sem.at[0, p, o - 1],
            recv_sem=first_sem.at[1, p, o - 1],
            device_id={"node": ahead(o)},
            device_id_type=MESH,
        )

    def packed(o):
        return pltpu.make_async_remote_copy(
            src_ref=pack_out.at[o - 1],
            dst_ref=pack_in.at[o - 1],
            send_sem=pack_sem.at[0, o - 1],
            recv_sem=pack_sem.at[1, o - 1],
            device_id={"node": ahead(o)},
            device_id_type=MESH,
        )

    def second(s, p, o):
        start, size = pieces[p]
        return pltpu.make_async_remote_copy(
            src_ref=mixed.at[o - 1, s, :, pl.ds(start, size)],
            dst_ref=side.at[s, mine, pl.ds(TOP + start, size)],
            send_sem=second_sem.at[0, s, p, o - 1],
            recv_sem=second_sem.at[1, s, p, o - 1],
            device_id={"node": ahead(o)},
            device_id_type=MESH,
        )

    order = tuple(range(nodes - 1, 0, -1))
    lane = lax.broadcasted_iota(jnp.int32, (EDGE, LANES), 1)

    def chunk_arrived(i):
        start, size = chunks[i]
        arrived_in(sec.at[:, :, pl.ds(TOP + start, size)], local_sem.at[i])

    chunk_arrived(0)
    chunk_arrived(1)
    pl.semaphore_wait(barrier, nodes - 1 + spaces - 1)
    for p in range(2):
        for o in order:
            first(p, o).start()
    for s in range(2):
        for way in range(2):
            halo(sec, halo_sem, s, way).start()
    chunk_arrived(2)
    chunk_arrived(3)

    groups = rows // EDGE
    for o in order:
        left = (ahead(o) * block + cols - 1) % cols
        right = (ahead(o) * block + block) % cols
        for s in range(2):
            pack = jnp.zeros((EDGE, LANES), jnp.float32)
            for g in range(groups):
                at = pl.ds(TOP + g * EDGE, EDGE)
                both = jnp.where(lane == LANES - 1, sec[s, left, at, :], sec[s, right, at, :])
                pack = jnp.where(lane // 2 == g, pltpu.roll(both, 2 * g + 1, 1), pack)
            pack_out[o - 1, s] = pack
        packed(o).start()
    for p in range(2, 4):
        for o in order:
            first(p, o).start()

    arrived_in(feed, local_sem.at[4])
    arrived_in(kill, local_sem.at[5])
    arrived_in(init, local_sem.at[6])

    for o in order:
        for p in range(2):
            first(p, o).wait_recv()
        for s in range(2):
            for way in range(2):
                forward(o, s, way).start()
    for o in order:
        packed(o).wait_recv()
        for s in range(2):
            pack = pack_in[o - 1, s]
            for g in range(groups):
                at = pl.ds(TOP + g * EDGE, EDGE)
                both = pltpu.roll(pack, LANES - 1 - 2 * g, 1)
                other[o - 1, s, 0, at, :] = both
                other[o - 1, s, block + 1, at, :] = both
    for s in range(2):
        for way in range(2):
            halo(sec, halo_sem, s, way).wait_recv()
    for o in order:
        for s in range(2):
            for way in range(2):
                forward(o, s, way).wait_recv()

    diffs = (diff_u, diff_v)
    sources = [me] + [ahead(negated(o)) for o in range(1, nodes)]
    targets = [me] + [ahead(o) for o in range(1, nodes)]
    weights = [[table[m * nodes + j] for j in sources] for m in targets]
    steps = [table[nodes * nodes + m] for m in targets]
    inverses = [
        [table[nodes * nodes + (1 + s) * nodes + m] for m in targets] for s in range(2)
    ]

    def ringed(left, middle, right, start):
        at = pl.ds(TOP + start, EDGE)
        here_tile = middle[at, :]
        before = pltpu.roll(jnp.where(lane == LANES - 1, left[at, :], here_tile), 1, 1)
        after = pltpu.roll(jnp.where(lane == 0, right[at, :], here_tile), LANES - 1, 1)
        below = middle[pl.ds(TOP + start + 1, EDGE), :]
        above = middle[pl.ds(TOP + start - 1, EDGE), :]
        return here_tile, (below + above) + (after + before)

    def mix(starts, worst):
        def one(c, worst):
            here_column = own + c
            left = (own + c + cols - 1) % cols
            right = (own + c + 1) % cols
            for start in starts:
                at = pl.ds(start, EDGE)
                f = feed[c, at, :]
                both_rates = f + kill[c, at, :]
                fields, laps, slopes = ([], []), ([], []), ([], [])
                for slot in range(nodes):
                    for s in range(2):
                        if slot == 0:
                            tiles = [sec.at[s, k] for k in (left, here_column, right)]
                        else:
                            tiles = [other.at[slot - 1, s, c + k] for k in range(3)]
                        w, ring = ringed(*tiles, start)
                        fields[s].append(w)
                        laps[s].append(diffs[s] * (ring - 4.0 * w))
                    u, v = fields[0][slot], fields[1][slot]
                    product = u * v * v
                    slopes[0].append(laps[0][slot] + (f * (1.0 - u) - product))
                    slopes[1].append(laps[1][slot] + (product - both_rates * v))
                for s in range(2):
                    base = init[s, c, at, :]
                    for t in range(nodes):
                        to = negated(t)
                        total = weights[t][0] * slopes[s][0]
                        for j in range(1, nodes):
                            total = total + weights[t][j] * slopes[s][j]
                        total = base + total
                        worst = jnp.maximum(worst, jnp.abs(total - fields[s][to]))
                        value = (total - steps[t] * laps[s][to]) * inverses[s][t]
                        if t == 0:
                            side[s, here_column, pl.ds(TOP + start, EDGE), :] = value
                        else:
                            mixed[t - 1, s, c, at, :] = value
            return worst

        return lax.fori_loop(0, block, one, worst)

    def send_back(s, ps):
        for p in ps:
            for o in order:
                second(s, p, o).start()

    def starts_of(ps):
        return [low for p in ps for low in range(pieces[p][0], sum(pieces[p]), EDGE)]

    worst = jnp.zeros((EDGE, LANES), jnp.float32)
    worst = mix(starts_of((0, 1)), worst)
    send_back(0, (0, 1))
    for o in order:
        first(2, o).wait_recv()
    worst = mix(starts_of((2,)), worst)
    send_back(0, (2,))
    for o in order:
        first(3, o).wait_recv()
    worst = mix(starts_of((3, 4)), worst)
    peak[0] = worst

    def peak_node(o):
        return pltpu.make_async_remote_copy(
            src_ref=peak.at[0],
            dst_ref=peaks_node.at[o - 1],
            send_sem=peak_node_sem.at[0, o - 1],
            recv_sem=peak_node_sem.at[1, o - 1],
            device_id={"node": ahead(o)},
            device_id_type=MESH,
        )

    def peak_space(o):
        return pltpu.make_async_remote_copy(
            src_ref=peak.at[1],
            dst_ref=peaks_space.at[o - 1],
            send_sem=peak_space_sem.at[0, o - 1],
            recv_sem=peak_space_sem.at[1, o - 1],
            device_id={"space": (here + o) % spaces},
            device_id_type=MESH,
        )

    for o in range(1, nodes):
        peak_node(o).start()
    send_back(0, (3, 4))
    send_back(1, range(len(pieces)))

    inverse = [inverses[s][0] for s in range(2)]
    factor = [steps[0] * diffs[s] * inverse[s] for s in range(2)]

    def around(ref, s, start, size):
        narrow = lax.broadcasted_iota(jnp.int32, (size, LANES), 1)
        at = pl.ds(start, size)
        tiles = [ref[s, k, at, :] for k in range(cols)]
        sums = []
        for k in range(cols):
            before, tile, after = tiles[k - 1], tiles[k], tiles[(k + 1) % cols]
            left = pltpu.roll(jnp.where(narrow == LANES - 1, before, tile), 1, 1)
            right = pltpu.roll(jnp.where(narrow == 0, after, tile), LANES - 1, 1)
            below = ref[s, k, pl.ds(start + 1, size), :]
            above = ref[s, k, pl.ds(start - 1, size), :]
            sums.append((below + above) + (right + left))
        return sums

    def band(s, spans):
        for k, (start, stop) in enumerate(spans):
            source, plane = (sec, s) if k == 0 else (works[k - 1], 0)
            for low in range(TOP + start, TOP + stop, EDGE):
                size = min(EDGE, TOP + stop - low)
                sums = around(source, plane, low, size)
                for c in range(cols):
                    value = side[s, c, pl.ds(low, size), :] + factor[s] * sums[c]
                    if k == SWEEPS - 1:
                        out[s, (low - TOP) // EDGE, c] = value
                    else:
                        works[k][0, c, pl.ds(low, size), :] = value

    reach = SWEEPS - 1
    cut = rows - 4 * EDGE
    late = rows - 2 * EDGE
    lower = [(k - reach, cut + reach - k - EDGE) for k in range(SWEEPS)]
    middle = [(cut + reach - k - EDGE, late - k) for k in range(reach)] + [(cut - EDGE, cut + EDGE)]
    upper = [(late + EDGE + k, rows + reach - k) for k in range(reach)]
    last = [(late - k, late + EDGE + k) for k in range(reach)] + [(cut + EDGE, rows)]

    def returned(s, p):
        for o in order:
            second(s, p, o).wait_recv()

    for s in range(2):
        returned(s, 0)
        returned(s, 1)
        for way in range(2):
            halo(side, side_sem, s, way).start()
        if s == 0:
            for o in range(1, nodes):
                peak_node(o).wait_recv()
            peak[1] = jnp.maximum(peak[0], jnp.max(peaks_node[...], axis=0))
            for o in range(1, spaces):
                peak_space(o).start()
        returned(s, 2)
        for way in range(2):
            halo(side, side_sem, s, way).wait_recv()
        band(s, lower)
        returned(s, 3)
        band(s, upper)
        band(s, middle)
        if s == 1:
            for o in range(1, spaces):
                peak_space(o).wait_recv()
            residual[0, 0] = jnp.max(jnp.maximum(peak[1], jnp.max(peaks_space[...], axis=0)))
        returned(s, 4)
        band(s, last)

    for o in order:
        packed(o).wait_send()
        for p in range(len(chunks)):
            first(p, o).wait_send()
    for s in range(2):
        for way in range(2):
            halo(sec, halo_sem, s, way).wait_send()
            halo(side, side_sem, s, way).wait_send()
            for o in order:
                forward(o, s, way).wait_send()
        for p in range(len(pieces)):
            for o in order:
                second(s, p, o).wait_send()
    for o in range(1, nodes):
        peak_node(o).wait_send()
    for o in range(1, spaces):
        peak_space(o).wait_send()


def shards(initial, sections, feed_rate, kill_rate):
    nodes = lax.axis_size("node")
    spaces = lax.axis_size("space")
    rows, columns = feed_rate.shape
    cols = columns // LANES
    block = cols // nodes
    points, quad_matrix = radau_table(nodes)
    steps = step_size * np.float32(points)
    table = np.concatenate(
        [
            step_size * np.float32(quad_matrix).reshape(-1),
            steps,
            1.0 / (4.0 * (steps * diff_u) + 1.0),
            1.0 / (4.0 * (steps * diff_v) + 1.0),
        ]
    ).astype(np.float32)
    high = TOP + rows + TOP
    f32 = jnp.float32

    def tiled(array):
        split = array.reshape(*array.shape[:-2], rows // EDGE, EDGE, cols, LANES)
        return jnp.swapaxes(split, -3, -2)

    any_spec = pl.BlockSpec(memory_space=pl.ANY)
    dma = pltpu.SemaphoreType.DMA
    result, residual = pl.pallas_call(
        functools.partial(kernel, nodes, spaces),
        out_shape=(
            pltpu.VMEM((2, rows // EDGE, cols, EDGE, LANES), f32),
            jax.ShapeDtypeStruct((1, 1), f32),
        ),
        in_specs=[pl.BlockSpec(memory_space=pltpu.SMEM)] + [any_spec] * 4,
        out_specs=(pl.BlockSpec(memory_space=pltpu.VMEM), pl.BlockSpec(memory_space=pltpu.SMEM)),
        scratch_shapes=[
            pltpu.VMEM((2, cols, high, LANES), f32),
            pltpu.VMEM((block, rows, LANES), f32),
            pltpu.VMEM((block, rows, LANES), f32),
            pltpu.VMEM((2, block, rows, LANES), f32),
            pltpu.VMEM((nodes - 1, 2, block + 2, high, LANES), f32),
            pltpu.VMEM((nodes - 1, 2, EDGE, LANES), f32),
            pltpu.VMEM((nodes - 1, 2, EDGE, LANES), f32),
            pltpu.VMEM((nodes - 1, 2, block, rows, LANES), f32),
            pltpu.VMEM((2, cols, high, LANES), f32),
            *[pltpu.VMEM((1, cols, high, LANES), f32)] * (SWEEPS - 1),
            pltpu.VMEM((2, EDGE, LANES), f32),
            pltpu.VMEM((nodes - 1, EDGE, LANES), f32),
            pltpu.VMEM((spaces - 1, EDGE, LANES), f32),
            dma((7,)),
            dma((2, 2, 2)),
            dma((nodes - 1, 2, 2, 2)),
            dma((2, nodes - 1)),
            dma((2, 4, nodes - 1)),
            dma((2, 2, 5, nodes - 1)),
            dma((2, 2, 2)),
            dma((2, nodes - 1)),
            dma((2, spaces - 1)),
        ],
        compiler_params=pltpu.CompilerParams(
            collective_id=0, has_side_effects=True, vmem_limit_bytes=61 * 1024 * 1024
        ),
    )(jnp.asarray(table), *[tiled(a) for a in (sections[0], feed_rate, kill_rate, initial)])
    result = jnp.swapaxes(result, -3, -2).reshape(sections.shape)
    return (result, residual.reshape(()))


def solution(mesh):
    placed = (
        P(None, "space", None),
        P("node", None, "space", None),
        P("space", None),
        P("space", None),
    )
    return jax.shard_map(
        shards,
        mesh=mesh,
        in_specs=placed,
        out_specs=(P("node", None, "space", None), P()),
        check_vma=False,
    )
```

time: 66.3 us -> 62.7 us (0.946)
  Pallas kernels: 62.5 us -> 58.9 us
    pallas_call x1, Pallas kernels: 62.5 us -> 58.9 us  [shards(): pl.pallas_call(functools.partial(kernel, nodes, spaces), out_shape=(pltpu...]
where the time goes in v1:
time: 62.7 us; the launch traced here: 62.5 us
  Pallas kernels  58.9 us (94%)
  between operations  2.33 us (4%)
  local copies, waits for them, and re-layouts  1.32 us (2%)
    pallas_call x1, Pallas kernels, shards(): pl.pallas_call(functools.partial(kernel, nodes, spaces), out_shape=(pltpu...  58.9 us
    unnamed x1, local copies, waits for them, and re-layouts  1.32 us

profile of v1, /device:TPU:0, one launch (start us, length us, event | category | flops | bytes accessed | tf_op | source)
XLA Modules:
  0.0 62.5 jit_solution(4712870163447927019)
XLA Ops:
  0.6 58.9 %shard_map.68 = (f32[2,8,32,8,128]{4,3,2,1,0:T(8,128)S(1)}, f32[1,1]{1,0:T(1,128)}) custom-call(f32[28]{0:T(128)} %constant.2.clone.table, f32[2,8,32,8,128]{4,3,2,1,0:T(8,128)} %bitcast.17, f32[8,32,8,128]{3,2,1,0:T(8,128)} %bitcast.19, f32[8,32,8,128]{3,2,1,0:T(8,128)} %bitcast.20, f32[2,8,32,8,128]{4,3,2,1,0:T(8,128)} %bitcast.18), custom_call_target="tpu_custom_call" | custom-call | tf_op jit(solution)/shard_map/pallas_call | solution.py:508
  59.5 1.3 %copy.9 = f32[1,2,64,4096]{3,2,1,0:T(8,128)} copy(f32[1,2,64,4096]{3,2,1,0:T(8,128)S(1)} %bitcast.16) | data formatting | bytes 4194304

commit v2 on v1

--- a/solution.py
+++ b/solution.py
@@ -143,8 +143,11 @@
     )
     own = me * block
 
+    def moved(m, o):
+        return ((m // wide + o // wide) % tall) * wide + (m % wide + o % wide) % wide
+
     def ahead(o):
-        return ((me // wide + o // wide) % tall) * wide + (me % wide + o % wide) % wide
+        return moved(me, o)
 
     def negated(o):
         return ((tall - o // wide) % tall) * wide + (wide - o % wide) % wide
@@ -291,13 +294,21 @@
                 forward(o, s, way).wait_recv()
 
     diffs = (diff_u, diff_v)
-    sources = [me] + [ahead(negated(o)) for o in range(1, nodes)]
-    targets = [me] + [ahead(o) for o in range(1, nodes)]
-    weights = [[table[m * nodes + j] for j in sources] for m in targets]
-    steps = [table[nodes * nodes + m] for m in targets]
-    inverses = [
-        [table[nodes * nodes + (1 + s) * nodes + m] for m in targets] for s in range(2)
+
+    def chosen(entries):
+        value = jnp.float32(entries[0])
+        for m in range(1, nodes):
+            value = jnp.where(me == m, jnp.float32(entries[m]), value)
+        return value
+
+    every = range(nodes)
+    quads, step_table, inverse_table = table
+    weights = [
+        [chosen([quads[moved(m, t), moved(m, negated(j))] for m in every]) for j in every]
+        for t in every
     ]
+    steps = [chosen([step_table[moved(m, t)] for m in every]) for t in every]
+    inverses = [[chosen([inverse_table[s][moved(m, t)] for m in every]) for t in every] for s in range(2)]
 
     def ringed(left, middle, right, start):
         at = pl.ds(TOP + start, EDGE)
@@ -457,7 +468,9 @@
         if s == 1:
             for o in range(1, spaces):
                 peak_space(o).wait_recv()
-            residual[0, 0] = jnp.max(jnp.maximum(peak[1], jnp.max(peaks_space[...], axis=0)))
+            residual[...] = jnp.max(
+                jnp.maximum(peak[1], jnp.max(peaks_space[...], axis=0)), keepdims=True
+            )
         returned(s, 4)
         band(s, last)
 
@@ -488,14 +501,11 @@
     block = cols // nodes
     points, quad_matrix = radau_table(nodes)
     steps = step_size * np.float32(points)
-    table = np.concatenate(
-        [
-            step_size * np.float32(quad_matrix).reshape(-1),
-            steps,
-            1.0 / (4.0 * (steps * diff_u) + 1.0),
-            1.0 / (4.0 * (steps * diff_v) + 1.0),
-        ]
-    ).astype(np.float32)
+    table = (
+        step_size * np.float32(quad_matrix),
+        steps,
+        [1.0 / (4.0 * (steps * diff) + 1.0) for diff in (diff_u, diff_v)],
+    )
     high = TOP + rows + TOP
     f32 = jnp.float32
 
@@ -506,13 +516,13 @@
     any_spec = pl.BlockSpec(memory_space=pl.ANY)
     dma = pltpu.SemaphoreType.DMA
     result, residual = pl.pallas_call(
-        functools.partial(kernel, nodes, spaces),
+        functools.partial(kernel, nodes, spaces, table),
         out_shape=(
             pltpu.VMEM((2, rows // EDGE, cols, EDGE, LANES), f32),
-            jax.ShapeDtypeStruct((1, 1), f32),
+            pltpu.VMEM((1, 1), f32),
         ),
-        in_specs=[pl.BlockSpec(memory_space=pltpu.SMEM)] + [any_spec] * 4,
-        out_specs=(pl.BlockSpec(memory_space=pltpu.VMEM), pl.BlockSpec(memory_space=pltpu.SMEM)),
+        in_specs=[any_spec] * 4,
+        out_specs=(pl.BlockSpec(memory_space=pltpu.VMEM), pl.BlockSpec(memory_space=pltpu.VMEM)),
         scratch_shapes=[
             pltpu.VMEM((2, cols, high, LANES), f32),
             pltpu.VMEM((block, rows, LANES), f32),
@@ -540,7 +550,7 @@
         compiler_params=pltpu.CompilerParams(
             collective_id=0, has_side_effects=True, vmem_limit_bytes=61 * 1024 * 1024
         ),
-    )(jnp.asarray(table), *[tiled(a) for a in (sections[0], feed_rate, kill_rate, initial)])
+    )(*[tiled(a) for a in (sections[0], feed_rate, kill_rate, initial)])
     result = jnp.swapaxes(result, -3, -2).reshape(sections.shape)
     return (result, residual.reshape(()))
 

time: 62.7 us -> 61 us (0.973)
  Pallas kernels: 58.9 us -> 57.7 us
    pallas_call x1, Pallas kernels: 58.9 us -> 57.7 us  [shards(): pl.pallas_call(functools.partial(kernel, nodes, spaces, table), out_shape...]
where the time goes in v2:
time: 61 us; the launch traced here: 60.8 us
  Pallas kernels  57.7 us (95%)
  between operations  1.8 us (3%)
  local copies, waits for them, and re-layouts  1.32 us (2%)
    pallas_call x1, Pallas kernels, shards(): pl.pallas_call(functools.partial(kernel, nodes, spaces, table), out_shape...  57.7 us
    unnamed x1, local copies, waits for them, and re-layouts  1.32 us

profile of v2, /device:TPU:0, one launch (start us, length us, event | category | flops | bytes accessed | tf_op | source)
XLA Modules:
  0.0 60.8 jit_solution(8727263138846281128)
XLA Ops:
  0.6 57.7 %shard_map.59 = (f32[2,8,32,8,128]{4,3,2,1,0:T(8,128)S(1)}, f32[1,1]{1,0:T(1,128)S(1)}) custom-call(f32[2,8,32,8,128]{4,3,2,1,0:T(8,128)} %bitcast.17, f32[8,32,8,128]{3,2,1,0:T(8,128)} %bitcast.19, f32[8,32,8,128]{3,2,1,0:T(8,128)} %bitcast.20, f32[2,8,32,8,128]{4,3,2,1,0:T(8,128)} %bitcast.18), custom_call_target="tpu_custom_call" | custom-call | tf_op jit(solution)/shard_map/pallas_call | solution.py:518
  58.4 1.3 %copy.8 = f32[1,2,64,4096]{3,2,1,0:T(8,128)} copy(f32[1,2,64,4096]{3,2,1,0:T(8,128)S(1)} %bitcast.16) | data formatting | bytes 4194304

commit v3 on v2

--- a/solution.py
+++ b/solution.py
@@ -83,6 +83,22 @@
 TOP = 2 * EDGE
 
 
+def ringed_sums(ref, s, start, size):
+    cols = ref.shape[1]
+    narrow = lax.broadcasted_iota(jnp.int32, (size, LANES), 1)
+    at = pl.ds(start, size)
+    tiles = [ref[s, k, at, :] for k in range(cols)]
+    sums = []
+    for k in range(cols):
+        before, tile, after = tiles[k - 1], tiles[k], tiles[(k + 1) % cols]
+        left = pltpu.roll(jnp.where(narrow == LANES - 1, before, tile), 1, 1)
+        right = pltpu.roll(jnp.where(narrow == 0, after, tile), LANES - 1, 1)
+        below = ref[s, k, pl.ds(start + 1, size), :]
+        above = ref[s, k, pl.ds(start - 1, size), :]
+        sums.append((below + above) + (right + left))
+    return sums
+
+
 def kernel(
     nodes,
     spaces,
@@ -92,7 +108,13 @@
     kill_rate,
     initial,
     out,
-    residual,
+    worst_out,
+    side,
+    works_a,
+    works_b,
+    works_c,
+    works_d,
+    works_e,
     sec,
     feed,
     kill,
@@ -101,24 +123,16 @@
     pack_out,
     pack_in,
     mixed,
-    side,
-    works_a,
-    works_b,
-    works_c,
-    works_d,
-    works_e,
     peak,
     peaks_node,
     peaks_space,
     local_sem,
-    halo_sem,
-    other_sem,
-    pack_sem,
+    send_sem,
     first_sem,
     second_sem,
     side_sem,
-    peak_node_sem,
-    peak_space_sem,
+    peak_sem,
+    misc_sem,
 ):
     works = (works_a, works_b, works_c, works_d, works_e)
     cols = sec.shape[1]
@@ -163,40 +177,45 @@
 
     for i, (start, size) in enumerate(chunks):
         for s in range(2):
-            fetch(sections.at[s], sec.at[s], start, size, TOP, local_sem.at[i])
+            fetch(sections.at[s], sec.at[s], start, size, TOP, local_sem.at[i // 2])
 
     barrier = pltpu.get_barrier_semaphore()
     for o in range(1, nodes):
         pl.semaphore_signal(barrier, inc=1, device_id={"node": ahead(o)}, device_id_type=MESH)
-    for o in range(1, spaces):
+    for o in (1, spaces - 1):
         pl.semaphore_signal(
             barrier, inc=1, device_id={"space": (here + o) % spaces}, device_id_type=MESH
         )
 
     mine = pl.ds(own, block)
-    fetch(feed_rate.at[:, mine], feed, 0, rows, 0, local_sem.at[4])
-    fetch(kill_rate.at[:, mine], kill, 0, rows, 0, local_sem.at[5])
+    fetch(feed_rate.at[:, mine], feed, 0, rows, 0, local_sem.at[2])
+    fetch(kill_rate.at[:, mine], kill, 0, rows, 0, local_sem.at[2])
     for s in range(2):
-        fetch(initial.at[s, :, mine], init.at[s], 0, rows, 0, local_sem.at[6])
-
-    def along(ref, sem, way):
+        fetch(initial.at[s, :, mine], init.at[s], 0, rows, 0, local_sem.at[3])
+
+    def along(ref, sent, received, way):
         start = TOP + rows - EDGE if way == 0 else TOP
         land = TOP - EDGE if way == 0 else TOP + rows
         target = (here + 1) % spaces if way == 0 else (here + spaces - 1) % spaces
         return pltpu.make_async_remote_copy(
             src_ref=ref.at[:, pl.ds(start, EDGE)],
             dst_ref=ref.at[:, pl.ds(land, EDGE)],
-            send_sem=sem.at[0, way],
-            recv_sem=sem.at[1, way],
+            send_sem=sent,
+            recv_sem=received,
             device_id={"space": target},
             device_id_type=MESH,
         )
 
-    def halo(ref, sem, s, way):
-        return along(ref.at[s], sem.at[s], way)
+    def sec_halo(s, way):
+        return along(sec.at[s], send_sem.at[0], misc_sem.at[0], way)
+
+    def side_halo(s, way):
+        return along(side.at[s], send_sem.at[1], side_sem.at[s], way)
 
     def forward(o, s, way):
-        return along(other.at[o - 1, s, pl.ds(1, block)], other_sem.at[o - 1, s], way)
+        return along(
+            other.at[o - 1, s, pl.ds(1, block)], send_sem.at[2], misc_sem.at[1], way
+        )
 
     def first(p, o):
         start, size = chunks[p]
@@ -204,8 +223,8 @@
         return pltpu.make_async_remote_copy(
             src_ref=sec.at[:, pl.ds(ahead(o) * block, block), where],
             dst_ref=other.at[o - 1, :, pl.ds(1, block), where],
-            send_sem=first_sem.at[0, p, o - 1],
-            recv_sem=first_sem.at[1, p, o - 1],
+            send_sem=send_sem.at[3],
+            recv_sem=first_sem.at[max(p - 1, 0)],
             device_id={"node": ahead(o)},
             device_id_type=MESH,
         )
@@ -214,8 +233,8 @@
         return pltpu.make_async_remote_copy(
             src_ref=pack_out.at[o - 1],
             dst_ref=pack_in.at[o - 1],
-            send_sem=pack_sem.at[0, o - 1],
-            recv_sem=pack_sem.at[1, o - 1],
+            send_sem=send_sem.at[4],
+            recv_sem=misc_sem.at[2],
             device_id={"node": ahead(o)},
             device_id_type=MESH,
         )
@@ -225,8 +244,8 @@
         return pltpu.make_async_remote_copy(
             src_ref=mixed.at[o - 1, s, :, pl.ds(start, size)],
             dst_ref=side.at[s, mine, pl.ds(TOP + start, size)],
-            send_sem=second_sem.at[0, s, p, o - 1],
-            recv_sem=second_sem.at[1, s, p, o - 1],
+            send_sem=send_sem.at[5],
+            recv_sem=second_sem.at[s, max(p - 1, 0)],
             device_id={"node": ahead(o)},
             device_id_type=MESH,
         )
@@ -234,21 +253,15 @@
     order = tuple(range(nodes - 1, 0, -1))
     lane = lax.broadcasted_iota(jnp.int32, (EDGE, LANES), 1)
 
-    def chunk_arrived(i):
-        start, size = chunks[i]
-        arrived_in(sec.at[:, :, pl.ds(TOP + start, size)], local_sem.at[i])
-
-    chunk_arrived(0)
-    chunk_arrived(1)
-    pl.semaphore_wait(barrier, nodes - 1 + spaces - 1)
+    arrived_in(sec.at[:, :, pl.ds(TOP, 2 * TOP)], local_sem.at[0])
+    pl.semaphore_wait(barrier, nodes - 1 + 2)
     for p in range(2):
         for o in order:
             first(p, o).start()
     for s in range(2):
         for way in range(2):
-            halo(sec, halo_sem, s, way).start()
-    chunk_arrived(2)
-    chunk_arrived(3)
+            sec_halo(s, way).start()
+    arrived_in(sec.at[:, :, pl.ds(TOP, rows - 2 * TOP)], local_sem.at[1])
 
     groups = rows // EDGE
     for o in order:
@@ -266,18 +279,19 @@
         for o in order:
             first(p, o).start()
 
-    arrived_in(feed, local_sem.at[4])
-    arrived_in(kill, local_sem.at[5])
-    arrived_in(init, local_sem.at[6])
-
+    arrived_in(init, local_sem.at[2])
+    arrived_in(init, local_sem.at[3])
+
+    def first_arrived(p, size):
+        arrived_in(other.at[:, :, pl.ds(1, block), pl.ds(TOP, size)], first_sem.at[p])
+
+    first_arrived(0, 2 * TOP)
     for o in order:
-        for p in range(2):
-            first(p, o).wait_recv()
         for s in range(2):
             for way in range(2):
                 forward(o, s, way).start()
+    arrived_in(pack_in, misc_sem.at[2])
     for o in order:
-        packed(o).wait_recv()
         for s in range(2):
             pack = pack_in[o - 1, s]
             for g in range(groups):
@@ -285,13 +299,8 @@
                 both = pltpu.roll(pack, LANES - 1 - 2 * g, 1)
                 other[o - 1, s, 0, at, :] = both
                 other[o - 1, s, block + 1, at, :] = both
-    for s in range(2):
-        for way in range(2):
-            halo(sec, halo_sem, s, way).wait_recv()
-    for o in order:
-        for s in range(2):
-            for way in range(2):
-                forward(o, s, way).wait_recv()
+    arrived_in(sec.at[:, :, pl.ds(0, 2 * EDGE)], misc_sem.at[0])
+    arrived_in(other.at[:, :, pl.ds(1, block), pl.ds(0, 2 * EDGE)], misc_sem.at[1])
 
     diffs = (diff_u, diff_v)
 
@@ -371,12 +380,10 @@
     worst = jnp.zeros((EDGE, LANES), jnp.float32)
     worst = mix(starts_of((0, 1)), worst)
     send_back(0, (0, 1))
-    for o in order:
-        first(2, o).wait_recv()
+    first_arrived(1, chunks[2][1])
     worst = mix(starts_of((2,)), worst)
     send_back(0, (2,))
-    for o in order:
-        first(3, o).wait_recv()
+    first_arrived(2, chunks[3][1])
     worst = mix(starts_of((3, 4)), worst)
     peak[0] = worst
 
@@ -384,21 +391,36 @@
         return pltpu.make_async_remote_copy(
             src_ref=peak.at[0],
             dst_ref=peaks_node.at[o - 1],
-            send_sem=peak_node_sem.at[0, o - 1],
-            recv_sem=peak_node_sem.at[1, o - 1],
+            send_sem=send_sem.at[6],
+            recv_sem=misc_sem.at[3],
             device_id={"node": ahead(o)},
             device_id_type=MESH,
         )
 
-    def peak_space(o):
+    def peak_space(k, way):
         return pltpu.make_async_remote_copy(
-            src_ref=peak.at[1],
-            dst_ref=peaks_space.at[o - 1],
-            send_sem=peak_space_sem.at[0, o - 1],
-            recv_sem=peak_space_sem.at[1, o - 1],
-            device_id={"space": (here + o) % spaces},
+            src_ref=peak.at[1 + k],
+            dst_ref=peaks_space.at[k, way],
+            send_sem=send_sem.at[7],
+            recv_sem=peak_sem.at[k],
+            device_id={"space": (here + (1, spaces - 1)[way]) % spaces},
             device_id_type=MESH,
         )
+
+    peak_steps = list(range(spaces // 2))
+    pace = -(-len(peak_steps) // 4)
+
+    def peak_start(k):
+        for way in range(2):
+            peak_space(k, way).start()
+
+    def peak_advance():
+        for k in peak_steps[:pace]:
+            arrived_in(peaks_space.at[k], peak_sem.at[k])
+            peak[2 + k] = jnp.maximum(peak[1 + k], jnp.max(peaks_space[k], axis=0))
+            if k + 1 < spaces // 2:
+                peak_start(k + 1)
+        del peak_steps[:pace]
 
     for o in range(1, nodes):
         peak_node(o).start()
@@ -408,33 +430,69 @@
     inverse = [inverses[s][0] for s in range(2)]
     factor = [steps[0] * diffs[s] * inverse[s] for s in range(2)]
 
-    def around(ref, s, start, size):
-        narrow = lax.broadcasted_iota(jnp.int32, (size, LANES), 1)
-        at = pl.ds(start, size)
-        tiles = [ref[s, k, at, :] for k in range(cols)]
-        sums = []
-        for k in range(cols):
-            before, tile, after = tiles[k - 1], tiles[k], tiles[(k + 1) % cols]
-            left = pltpu.roll(jnp.where(narrow == LANES - 1, before, tile), 1, 1)
-            right = pltpu.roll(jnp.where(narrow == 0, after, tile), LANES - 1, 1)
-            below = ref[s, k, pl.ds(start + 1, size), :]
-            above = ref[s, k, pl.ds(start - 1, size), :]
-            sums.append((below + above) + (right + left))
-        return sums
+    def put(s, k, low, size, values):
+        for c in range(cols):
+            if k == SWEEPS - 1:
+                out[s, (low - TOP) // EDGE, c] = values[c]
+            else:
+                works[k][0, c, pl.ds(low, size), :] = values[c]
+
+    def steps_in(span):
+        start, stop = span
+        return [(low, min(EDGE, TOP + stop - low)) for low in range(TOP + start, TOP + stop, EDGE)]
 
     def band(s, spans):
-        for k, (start, stop) in enumerate(spans):
+        for k, span in enumerate(spans):
             source, plane = (sec, s) if k == 0 else (works[k - 1], 0)
-            for low in range(TOP + start, TOP + stop, EDGE):
-                size = min(EDGE, TOP + stop - low)
-                sums = around(source, plane, low, size)
-                for c in range(cols):
-                    value = side[s, c, pl.ds(low, size), :] + factor[s] * sums[c]
-                    if k == SWEEPS - 1:
-                        out[s, (low - TOP) // EDGE, c] = value
-                    else:
-                        works[k][0, c, pl.ds(low, size), :] = value
-
+            for low, size in steps_in(span):
+                sums = ringed_sums(source, plane, low, size)
+                put(s, k, low, size, [
+                    side[s, c, pl.ds(low, size), :] + factor[s] * sums[c] for c in range(cols)
+                ])
+
+    lower, middle, upper, last = bands_of(rows)
+
+    def returned(s, p, size):
+        arrived_in(mixed.at[:, s, :, pl.ds(0, size)], second_sem.at[s, p - 1])
+
+    for s in range(2):
+        returned(s, 1, 2 * EDGE)
+        for way in range(2):
+            side_halo(s, way).start()
+        if s == 0:
+            arrived_in(peaks_node, misc_sem.at[3])
+            peak[1] = jnp.maximum(peak[0], jnp.max(peaks_node[...], axis=0))
+            peak_start(0)
+        returned(s, 2, pieces[2][1])
+        arrived_in(side.at[s, :, pl.ds(0, 2 * EDGE)], side_sem.at[s])
+        band(s, lower)
+        peak_advance()
+        band(s, upper)
+        returned(s, 3, pieces[3][1])
+        band(s, middle)
+        if s == 0:
+            peak_advance()
+            returned(s, 4, EDGE)
+            band(s, last)
+            peak_advance()
+        else:
+            worst_out[...] = jnp.full((EDGE, LANES), jnp.max(peak[1 + spaces // 2]))
+            for low, size in steps_in(last[0]):
+                sums = ringed_sums(sec, s, low, size)
+                put(s, 0, low, size, [factor[s] * total for total in sums])
+            returned(s, 4, EDGE)
+
+    arrived_in(sec.at[:, :, pl.ds(0, 2 * EDGE)], send_sem.at[0])
+    arrived_in(side.at[:, :, pl.ds(0, 2 * EDGE)], send_sem.at[1])
+    arrived_in(other.at[:, :, pl.ds(1, block), pl.ds(0, 2 * EDGE)], send_sem.at[2])
+    arrived_in(mixed, send_sem.at[3])
+    arrived_in(pack_out, send_sem.at[4])
+    arrived_in(mixed, send_sem.at[5])
+    arrived_in(peaks_node, send_sem.at[6])
+    arrived_in(peaks_space, send_sem.at[7])
+
+
+def bands_of(rows):
     reach = SWEEPS - 1
     cut = rows - 4 * EDGE
     late = rows - 2 * EDGE
@@ -442,55 +500,70 @@
     middle = [(cut + reach - k - EDGE, late - k) for k in range(reach)] + [(cut - EDGE, cut + EDGE)]
     upper = [(late + EDGE + k, rows + reach - k) for k in range(reach)]
     last = [(late - k, late + EDGE + k) for k in range(reach)] + [(cut + EDGE, rows)]
-
-    def returned(s, p):
-        for o in order:
-            second(s, p, o).wait_recv()
-
-    for s in range(2):
-        returned(s, 0)
-        returned(s, 1)
-        for way in range(2):
-            halo(side, side_sem, s, way).start()
-        if s == 0:
-            for o in range(1, nodes):
-                peak_node(o).wait_recv()
-            peak[1] = jnp.maximum(peak[0], jnp.max(peaks_node[...], axis=0))
-            for o in range(1, spaces):
-                peak_space(o).start()
-        returned(s, 2)
-        for way in range(2):
-            halo(side, side_sem, s, way).wait_recv()
-        band(s, lower)
-        returned(s, 3)
-        band(s, upper)
-        band(s, middle)
-        if s == 1:
-            for o in range(1, spaces):
-                peak_space(o).wait_recv()
-            residual[...] = jnp.max(
-                jnp.maximum(peak[1], jnp.max(peaks_space[...], axis=0)), keepdims=True
-            )
-        returned(s, 4)
-        band(s, last)
-
-    for o in order:
-        packed(o).wait_send()
-        for p in range(len(chunks)):
-            first(p, o).wait_send()
-    for s in range(2):
-        for way in range(2):
-            halo(sec, halo_sem, s, way).wait_send()
-            halo(side, side_sem, s, way).wait_send()
-            for o in order:
-                forward(o, s, way).wait_send()
-        for p in range(len(pieces)):
-            for o in order:
-                second(s, p, o).wait_send()
-    for o in range(1, nodes):
-        peak_node(o).wait_send()
-    for o in range(1, spaces):
-        peak_space(o).wait_send()
+    return lower, middle, upper, last
+
+
+def finish(
+    factors,
+    swept,
+    worst,
+    side,
+    in_a,
+    in_b,
+    in_c,
+    in_d,
+    in_e,
+    out,
+    residual,
+    works_a,
+    works_b,
+    works_c,
+    works_d,
+    works_e,
+    fresh,
+    single,
+    sem,
+):
+    works = (works_a, works_b, works_c, works_d, works_e)
+    groups, cols = swept.shape[1:3]
+    last = bands_of(groups * EDGE)[3]
+    done = last[-1][0] // EDGE
+    copies = [
+        pltpu.make_async_copy(swept.at[0], out.at[0], sem.at[0]),
+        pltpu.make_async_copy(swept.at[1, pl.ds(0, done)], out.at[1, pl.ds(0, done)], sem.at[1]),
+        pltpu.make_async_copy(single, residual, sem.at[2]),
+    ]
+    copies[0].start()
+    copies[1].start()
+    single[...] = worst[pl.ds(0, 1), pl.ds(0, 1)]
+    copies[2].start()
+    me = lax.axis_index("node")
+    factor = jnp.float32(factors[0])
+    for m in range(1, len(factors)):
+        factor = jnp.where(me == m, jnp.float32(factors[m]), factor)
+    for k, (start, stop) in enumerate(last):
+        for low in range(TOP + start, TOP + stop, EDGE):
+            size = min(EDGE, TOP + stop - low)
+            at = pl.ds(low, size)
+            if k == 0:
+                for c in range(cols):
+                    works[0][0, c, at, :] = works[0][0, c, at, :] + side[1, c, at, :]
+                continue
+            sums = ringed_sums(works[k - 1], 0, low, size)
+            for c in range(cols):
+                value = side[1, c, at, :] + factor * sums[c]
+                if k == SWEEPS - 1:
+                    fresh[(low - TOP) // EDGE - done, c] = value
+                else:
+                    works[k][0, c, at, :] = value
+            if k == SWEEPS - 1:
+                g = (low - TOP) // EDGE
+                copies.append(
+                    pltpu.make_async_copy(fresh.at[g - done], out.at[1, g], sem.at[3 + g - done])
+                )
+                copies[-1].start()
+    for copy in copies:
+        copy.wait()
 
 
 def shards(initial, sections, feed_rate, kill_rate):
@@ -508,6 +581,7 @@
     )
     high = TOP + rows + TOP
     f32 = jnp.float32
+    factors = steps * diff_v * table[2][1]
 
     def tiled(array):
         split = array.reshape(*array.shape[:-2], rows // EDGE, EDGE, cols, LANES)
@@ -515,14 +589,19 @@
 
     any_spec = pl.BlockSpec(memory_space=pl.ANY)
     dma = pltpu.SemaphoreType.DMA
-    result, residual = pl.pallas_call(
+    vmem = pl.BlockSpec(memory_space=pltpu.VMEM)
+    kept = (
+        pltpu.VMEM((2, rows // EDGE, cols, EDGE, LANES), f32),
+        pltpu.VMEM((EDGE, LANES), f32),
+        pltpu.VMEM((2, cols, high, LANES), f32),
+        *[pltpu.VMEM((1, cols, high, LANES), f32)] * (SWEEPS - 1),
+    )
+    room = 64 * 1024 * 1024 - 1024 * 1024 - sum(4 * int(np.prod(a.shape)) for a in kept)
+    held = pl.pallas_call(
         functools.partial(kernel, nodes, spaces, table),
-        out_shape=(
-            pltpu.VMEM((2, rows // EDGE, cols, EDGE, LANES), f32),
-            pltpu.VMEM((1, 1), f32),
-        ),
+        out_shape=kept,
         in_specs=[any_spec] * 4,
-        out_specs=(pl.BlockSpec(memory_space=pltpu.VMEM), pl.BlockSpec(memory_space=pltpu.VMEM)),
+        out_specs=(vmem,) * len(kept),
         scratch_shapes=[
             pltpu.VMEM((2, cols, high, LANES), f32),
             pltpu.VMEM((block, rows, LANES), f32),
@@ -532,25 +611,40 @@
             pltpu.VMEM((nodes - 1, 2, EDGE, LANES), f32),
             pltpu.VMEM((nodes - 1, 2, EDGE, LANES), f32),
             pltpu.VMEM((nodes - 1, 2, block, rows, LANES), f32),
-            pltpu.VMEM((2, cols, high, LANES), f32),
-            *[pltpu.VMEM((1, cols, high, LANES), f32)] * (SWEEPS - 1),
-            pltpu.VMEM((2, EDGE, LANES), f32),
+            pltpu.VMEM((2 + spaces // 2, EDGE, LANES), f32),
             pltpu.VMEM((nodes - 1, EDGE, LANES), f32),
-            pltpu.VMEM((spaces - 1, EDGE, LANES), f32),
-            dma((7,)),
-            dma((2, 2, 2)),
-            dma((nodes - 1, 2, 2, 2)),
-            dma((2, nodes - 1)),
-            dma((2, 4, nodes - 1)),
-            dma((2, 2, 5, nodes - 1)),
-            dma((2, 2, 2)),
-            dma((2, nodes - 1)),
-            dma((2, spaces - 1)),
+            pltpu.VMEM((spaces // 2, 2, EDGE, LANES), f32),
+            dma((4,)),
+            dma((8,)),
+            dma((3,)),
+            dma((2, 4)),
+            dma((2,)),
+            dma((spaces // 2,)),
+            dma((4,)),
         ],
         compiler_params=pltpu.CompilerParams(
-            collective_id=0, has_side_effects=True, vmem_limit_bytes=61 * 1024 * 1024
+            collective_id=0, has_side_effects=True, vmem_limit_bytes=room
         ),
     )(*[tiled(a) for a in (sections[0], feed_rate, kill_rate, initial)])
+    late = bands_of(rows)[3][-1]
+    fresh = (late[1] - late[0]) // EDGE
+    result, residual, *_ = pl.pallas_call(
+        functools.partial(finish, factors),
+        out_shape=(
+            jax.ShapeDtypeStruct(kept[0].shape, f32),
+            jax.ShapeDtypeStruct((1, 1), f32),
+            *kept[3:],
+        ),
+        in_specs=[vmem] * len(kept),
+        out_specs=(any_spec, any_spec, *[vmem] * (SWEEPS - 1)),
+        scratch_shapes=[
+            pltpu.VMEM((fresh, cols, EDGE, LANES), f32),
+            pltpu.VMEM((1, 1), f32),
+            dma((3 + fresh,)),
+        ],
+        input_output_aliases={3 + k: 2 + k for k in range(SWEEPS - 1)},
+        compiler_params=pltpu.CompilerParams(vmem_limit_bytes=16 * 1024 * 1024),
+    )(*held)
     result = jnp.swapaxes(result, -3, -2).reshape(sections.shape)
     return (result, residual.reshape(()))
 

time: 61 us -> 59.2 us (0.970)
  local copies, waits for them, and re-layouts: 1.32 us -> 0 us
  between operations: 1.8 us -> 0.64 us
  Pallas kernels: 57.7 us -> 58.4 us
    pallas_call x0 -> x1, Pallas kernels: none -> 1.68 us  [shards(): pl.pallas_call(functools.partial(finish, factors), out_shape=(jax.ShapeDt...]
    unnamed x1 -> x0, local copies, waits for them, and re-layouts: 1.32 us -> none
    pallas_call x1, Pallas kernels: 57.7 us -> 56.7 us  [shards(): pl.pallas_call(functools.partial(kernel, nodes, spaces, table), out_shape...]
where the time goes in v3:
time: 59.2 us; the launch traced here: 59.1 us
  Pallas kernels  58.4 us (99%)
  between operations  0.64 us (1%)
    pallas_call x1, Pallas kernels, shards(): pl.pallas_call(functools.partial(kernel, nodes, spaces, table), out_shape...  56.7 us
    pallas_call x1, Pallas kernels, shards(): pl.pallas_call(functools.partial(finish, factors), out_shape=(jax.ShapeDt...  1.68 us

profile of v3, /device:TPU:0, one launch (start us, length us, event | category | flops | bytes accessed | tf_op | source)
XLA Modules:
  0.0 59.1 jit_solution(12024278417464912768)
XLA Ops:
  0.6 56.7 %shard_map.59 = (f32[2,8,32,8,128]{4,3,2,1,0:T(8,128)S(1)}, f32[8,128]{1,0:T(8,128)S(1)}, f32[2,32,96,128]{3,2,1,0:T(8,128)S(1)}, f32[1,32,96,128]{3,2,1,0:T(8,1...) custom-call(f32[2,8,32,8,128]{4,3,2,1,0:T(8,128)} %bitcast.16, ...), custom_call_target="tpu_custom_call" | custom-call | tf_op jit(solution)/shard_map/pallas_call | solution.py:600
  57.4 1.7 %shard_map.60 = (f32[2,8,32,8,128]{4,3,2,1,0:T(8,128)}, f32[1,1]{1,0:T(1,128)}, f32[1,32,96,128]{3,2,1,0:T(8,128)S(1)}, f32[1,32,96,128]{3,2,1,0:T(8,128)S(1)}, ...) custom-call(f32[2,8,32,8,128]{4,3,2,1,0:T(8,128)S(1)} %get-tuple-ele, ...), custom_call_target="tpu_custom_call", output_to_operand_aliasing={{2}: (3, {}), {3}: (4, {}), {4}: (5, {}), {5}: (6, {}), {6}... | custom-call | tf_op jit(solution)/shard_map/pallas_call | solution.py:631

commit v4 on v3

--- a/solution.py
+++ b/solution.py
@@ -397,29 +397,27 @@
             device_id_type=MESH,
         )
 
-    def peak_space(k, way):
+    def peak_space(k):
+        apart = 2**k
         return pltpu.make_async_remote_copy(
             src_ref=peak.at[1 + k],
-            dst_ref=peaks_space.at[k, way],
+            dst_ref=peaks_space.at[k],
             send_sem=send_sem.at[7],
             recv_sem=peak_sem.at[k],
-            device_id={"space": (here + (1, spaces - 1)[way]) % spaces},
+            device_id={"space": here + apart - here // apart % 2 * 2 * apart},
             device_id_type=MESH,
         )
 
-    peak_steps = list(range(spaces // 2))
-    pace = -(-len(peak_steps) // 4)
-
-    def peak_start(k):
-        for way in range(2):
-            peak_space(k, way).start()
+    doublings = peaks_space.shape[0]
+    peak_steps = list(range(doublings))
+    pace = -(-doublings // 3)
 
     def peak_advance():
         for k in peak_steps[:pace]:
             arrived_in(peaks_space.at[k], peak_sem.at[k])
-            peak[2 + k] = jnp.maximum(peak[1 + k], jnp.max(peaks_space[k], axis=0))
-            if k + 1 < spaces // 2:
-                peak_start(k + 1)
+            peak[2 + k] = jnp.maximum(peak[1 + k], peaks_space[k])
+            if k + 1 < doublings:
+                peak_space(k + 1).start()
         del peak_steps[:pace]
 
     for o in range(1, nodes):
@@ -462,11 +460,15 @@
         if s == 0:
             arrived_in(peaks_node, misc_sem.at[3])
             peak[1] = jnp.maximum(peak[0], jnp.max(peaks_node[...], axis=0))
-            peak_start(0)
+            peak_space(0).start()
+        else:
+            peak_advance()
+            worst_out[...] = jnp.full((EDGE, LANES), jnp.max(peak[1 + doublings]))
         returned(s, 2, pieces[2][1])
         arrived_in(side.at[s, :, pl.ds(0, 2 * EDGE)], side_sem.at[s])
         band(s, lower)
-        peak_advance()
+        if s == 0:
+            peak_advance()
         band(s, upper)
         returned(s, 3, pieces[3][1])
         band(s, middle)
@@ -474,9 +476,7 @@
             peak_advance()
             returned(s, 4, EDGE)
             band(s, last)
-            peak_advance()
         else:
-            worst_out[...] = jnp.full((EDGE, LANES), jnp.max(peak[1 + spaces // 2]))
             for low, size in steps_in(last[0]):
                 sums = ringed_sums(sec, s, low, size)
                 put(s, 0, low, size, [factor[s] * total for total in sums])
@@ -572,6 +572,7 @@
     rows, columns = feed_rate.shape
     cols = columns // LANES
     block = cols // nodes
+    doublings = (spaces - 1).bit_length()
     points, quad_matrix = radau_table(nodes)
     steps = step_size * np.float32(points)
     table = (
@@ -611,15 +612,15 @@
             pltpu.VMEM((nodes - 1, 2, EDGE, LANES), f32),
             pltpu.VMEM((nodes - 1, 2, EDGE, LANES), f32),
             pltpu.VMEM((nodes - 1, 2, block, rows, LANES), f32),
-            pltpu.VMEM((2 + spaces // 2, EDGE, LANES), f32),
+            pltpu.VMEM((2 + doublings, EDGE, LANES), f32),
             pltpu.VMEM((nodes - 1, EDGE, LANES), f32),
-            pltpu.VMEM((spaces // 2, 2, EDGE, LANES), f32),
+            pltpu.VMEM((doublings, EDGE, LANES), f32),
             dma((4,)),
             dma((8,)),
             dma((3,)),
             dma((2, 4)),
             dma((2,)),
-            dma((spaces // 2,)),
+            dma((doublings,)),
             dma((4,)),
         ],
         compiler_params=pltpu.CompilerParams(

time: 59.2 us -> 55.2 us (0.932)
  Pallas kernels: 58.4 us -> 54.1 us
    pallas_call x1, Pallas kernels: 56.7 us -> 52.4 us  [shards(): pl.pallas_call(functools.partial(kernel, nodes, spaces, table), out_shape...]
where the time goes in v4:
time: 55.2 us; the launch traced here: 54.7 us
  Pallas kernels  54.1 us (98%)
  between operations  0.64 us (1%)
    pallas_call x1, Pallas kernels, shards(): pl.pallas_call(functools.partial(kernel, nodes, spaces, table), out_shape...  52.4 us
    pallas_call x1, Pallas kernels, shards(): pl.pallas_call(functools.partial(finish, factors), out_shape=(jax.ShapeDt...  1.68 us

profile of v4, /device:TPU:0, one launch (start us, length us, event | category | flops | bytes accessed | tf_op | source)
XLA Modules:
  0.0 54.7 jit_solution(16832037376414294032)
XLA Ops:
  0.6 52.4 %shard_map.59 = (f32[2,8,32,8,128]{4,3,2,1,0:T(8,128)S(1)}, f32[8,128]{1,0:T(8,128)S(1)}, f32[2,32,96,128]{3,2,1,0:T(8,128)S(1)}, f32[1,32,96,128]{3,2,1,0:T(8,1...) custom-call(f32[2,8,32,8,128]{4,3,2,1,0:T(8,128)} %bitcast.16, ...), custom_call_target="tpu_custom_call" | custom-call | tf_op jit(solution)/shard_map/pallas_call | solution.py:601
  53.0 1.7 %shard_map.60 = (f32[2,8,32,8,128]{4,3,2,1,0:T(8,128)}, f32[1,1]{1,0:T(1,128)}, f32[1,32,96,128]{3,2,1,0:T(8,128)S(1)}, f32[1,32,96,128]{3,2,1,0:T(8,128)S(1)}, ...) custom-call(f32[2,8,32,8,128]{4,3,2,1,0:T(8,128)S(1)} %get-tuple-ele, ...), custom_call_target="tpu_custom_call", output_to_operand_aliasing={{2}: (3, {}), {3}: (4, {}), {4}: (5, {}), {5}: (6, {}), {6}... | custom-call | tf_op jit(solution)/shard_map/pallas_call | solution.py:632

commit v5 on v4

--- a/solution.py
+++ b/solution.py
@@ -380,6 +380,7 @@
     worst = jnp.zeros((EDGE, LANES), jnp.float32)
     worst = mix(starts_of((0, 1)), worst)
     send_back(0, (0, 1))
+    send_back(1, (0, 1))
     first_arrived(1, chunks[2][1])
     worst = mix(starts_of((2,)), worst)
     send_back(0, (2,))
@@ -423,7 +424,7 @@
     for o in range(1, nodes):
         peak_node(o).start()
     send_back(0, (3, 4))
-    send_back(1, range(len(pieces)))
+    send_back(1, (2, 3, 4))
 
     inverse = [inverses[s][0] for s in range(2)]
     factor = [steps[0] * diffs[s] * inverse[s] for s in range(2)]
@@ -457,6 +458,14 @@
         returned(s, 1, 2 * EDGE)
         for way in range(2):
             side_halo(s, way).start()
+
+    for s in range(2):
+        arrived_in(side.at[s, :, pl.ds(0, 2 * EDGE)], side_sem.at[s])
+        band(s, upper)
+        if s == 1:
+            peak_advance()
+        returned(s, 2, pieces[2][1])
+        band(s, lower)
         if s == 0:
             arrived_in(peaks_node, misc_sem.at[3])
             peak[1] = jnp.maximum(peak[0], jnp.max(peaks_node[...], axis=0))
@@ -464,12 +473,6 @@
         else:
             peak_advance()
             worst_out[...] = jnp.full((EDGE, LANES), jnp.max(peak[1 + doublings]))
-        returned(s, 2, pieces[2][1])
-        arrived_in(side.at[s, :, pl.ds(0, 2 * EDGE)], side_sem.at[s])
-        band(s, lower)
-        if s == 0:
-            peak_advance()
-        band(s, upper)
         returned(s, 3, pieces[3][1])
         band(s, middle)
         if s == 0:

time: 55.2 us -> 54.9 us (level)
  no operation moved by 1% of the time
where the time goes in v5:
time: 54.9 us; the launch traced here: 54.8 us
  Pallas kernels  54.1 us (99%)
  between operations  0.64 us (1%)
    pallas_call x1, Pallas kernels, shards(): pl.pallas_call(functools.partial(kernel, nodes, spaces, table), out_shape...  52.4 us
    pallas_call x1, Pallas kernels, shards(): pl.pallas_call(functools.partial(finish, factors), out_shape=(jax.ShapeDt...  1.68 us

profile of v5, /device:TPU:0, one launch (start us, length us, event | category | flops | bytes accessed | tf_op | source)
XLA Modules:
  0.0 54.8 jit_solution(5530727140831947393)
XLA Ops:
  0.6 52.4 %shard_map.59 = (f32[2,8,32,8,128]{4,3,2,1,0:T(8,128)S(1)}, f32[8,128]{1,0:T(8,128)S(1)}, f32[2,32,96,128]{3,2,1,0:T(8,128)S(1)}, f32[1,32,96,128]{3,2,1,0:T(8,1...) custom-call(f32[2,8,32,8,128]{4,3,2,1,0:T(8,128)} %bitcast.16, ...), custom_call_target="tpu_custom_call" | custom-call | tf_op jit(solution)/shard_map/pallas_call | solution.py:604
  53.1 1.7 %shard_map.60 = (f32[2,8,32,8,128]{4,3,2,1,0:T(8,128)}, f32[1,1]{1,0:T(1,128)}, f32[1,32,96,128]{3,2,1,0:T(8,128)S(1)}, f32[1,32,96,128]{3,2,1,0:T(8,128)S(1)}, ...) custom-call(f32[2,8,32,8,128]{4,3,2,1,0:T(8,128)S(1)} %get-tuple-ele, ...), custom_call_target="tpu_custom_call", output_to_operand_aliasing={{2}: (3, {}), {3}: (4, {}), {4}: (5, {}), {5}: (6, {}), {6}... | custom-call | tf_op jit(solution)/shard_map/pallas_call | solution.py:635

commit v6 on v5

--- a/solution.py
+++ b/solution.py
@@ -175,10 +175,6 @@
     def arrived_in(ref, sem):
         pltpu.make_async_copy(ref, ref, sem).wait()
 
-    for i, (start, size) in enumerate(chunks):
-        for s in range(2):
-            fetch(sections.at[s], sec.at[s], start, size, TOP, local_sem.at[i // 2])
-
     barrier = pltpu.get_barrier_semaphore()
     for o in range(1, nodes):
         pl.semaphore_signal(barrier, inc=1, device_id={"node": ahead(o)}, device_id_type=MESH)
@@ -186,6 +182,10 @@
         pl.semaphore_signal(
             barrier, inc=1, device_id={"space": (here + o) % spaces}, device_id_type=MESH
         )
+
+    for i, (start, size) in enumerate(chunks):
+        for s in range(2):
+            fetch(sections.at[s], sec.at[s], start, size, TOP, local_sem.at[i // 2])
 
     mine = pl.ds(own, block)
     fetch(feed_rate.at[:, mine], feed, 0, rows, 0, local_sem.at[2])
@@ -369,6 +369,17 @@
 
         return lax.fori_loop(0, block, one, worst)
 
+    def edges(p, o):
+        start, size = pieces[p]
+        return pltpu.make_async_remote_copy(
+            src_ref=mixed.at[o - 1, :, :, pl.ds(start, size)],
+            dst_ref=side.at[:, mine, pl.ds(TOP + start, size)],
+            send_sem=send_sem.at[5],
+            recv_sem=second_sem.at[0, 0],
+            device_id={"node": ahead(o)},
+            device_id_type=MESH,
+        )
+
     def send_back(s, ps):
         for p in ps:
             for o in order:
@@ -379,8 +390,9 @@
 
     worst = jnp.zeros((EDGE, LANES), jnp.float32)
     worst = mix(starts_of((0, 1)), worst)
-    send_back(0, (0, 1))
-    send_back(1, (0, 1))
+    for p in range(2):
+        for o in order:
+            edges(p, o).start()
     first_arrived(1, chunks[2][1])
     worst = mix(starts_of((2,)), worst)
     send_back(0, (2,))
@@ -454,8 +466,8 @@
     def returned(s, p, size):
         arrived_in(mixed.at[:, s, :, pl.ds(0, size)], second_sem.at[s, p - 1])
 
+    arrived_in(mixed.at[:, :, :, pl.ds(0, 2 * EDGE)], second_sem.at[0, 0])
     for s in range(2):
-        returned(s, 1, 2 * EDGE)
         for way in range(2):
             side_halo(s, way).start()
 

time: 54.9 us -> 54.9 us (level)
  no operation moved by 1% of the time
where the time goes in v6:
time: 54.9 us; the launch traced here: 54.7 us
  Pallas kernels  54.1 us (99%)
  between operations  0.64 us (1%)
    pallas_call x1, Pallas kernels, shards(): pl.pallas_call(functools.partial(kernel, nodes, spaces, table), out_shape...  52.4 us
    pallas_call x1, Pallas kernels, shards(): pl.pallas_call(functools.partial(finish, factors), out_shape=(jax.ShapeDt...  1.68 us

profile of v6, /device:TPU:0, one launch (start us, length us, event | category | flops | bytes accessed | tf_op | source)
XLA Modules:
  0.0 54.7 jit_solution(17071709506557270333)
XLA Ops:
  0.6 52.4 %shard_map.59 = (f32[2,8,32,8,128]{4,3,2,1,0:T(8,128)S(1)}, f32[8,128]{1,0:T(8,128)S(1)}, f32[2,32,96,128]{3,2,1,0:T(8,128)S(1)}, f32[1,32,96,128]{3,2,1,0:T(8,1...) custom-call(f32[2,8,32,8,128]{4,3,2,1,0:T(8,128)} %bitcast.16, ...), custom_call_target="tpu_custom_call" | custom-call | tf_op jit(solution)/shard_map/pallas_call | solution.py:616
  53.1 1.7 %shard_map.60 = (f32[2,8,32,8,128]{4,3,2,1,0:T(8,128)}, f32[1,1]{1,0:T(1,128)}, f32[1,32,96,128]{3,2,1,0:T(8,128)S(1)}, f32[1,32,96,128]{3,2,1,0:T(8,128)S(1)}, ...) custom-call(f32[2,8,32,8,128]{4,3,2,1,0:T(8,128)S(1)} %get-tuple-ele, ...), custom_call_target="tpu_custom_call", output_to_operand_aliasing={{2}: (3, {}), {3}: (4, {}), {4}: (5, {}), {5}: (6, {}), {6}... | custom-call | tf_op jit(solution)/shard_map/pallas_call | solution.py:647
